TPU v7x, 512 devices: a whole 4x8x8 slice. The times are simulated.
512 devices in a mesh: gx: 4 (over x), gy: 8 (over z), gz: 16 (over y, core).
Axes of the slice: x: 4, y: 8, z: 8, core: 2. Of those that a mesh axis runs over, the one named last changes fastest.
Arguments:
- positions: float32 [3, 262144], P(None, ('gx', 'gy', 'gz')), may hold values from -6 to 6
- frames: float32 [128, 3, 4096], P(None, None, ('gy', 'gz')), may hold values from -6 to 6
- path_slot: int32 [512, 32], P(('gx', 'gy', 'gz')), may hold values from 0 to 511, as said below
- path_count: int32 [512], replicated, may hold values from 1 to 32, 4096 in all
- path_order: int32 [4096], replicated, may hold values from 0 to 4095, each once
- frame_rank: int32 [128], replicated, may hold values from 0 to 127, each once
Outputs:
- forces: float32 [3, 262144], P(None, ('gx', 'gy', 'gz'))
- path_cv: float32 [2], replicated
Inputs may be any that keep to these rules, and one draw needn't show every extreme that they name: `path_slot`: within one domain's row the 32 local atom indices are all different.
All inputs are finite; a program needn't handle non-finite values.
Results may differ from a plain program's by a relative error of at most 0.00013.
Values sent between devices are 32-bit elements; how exact they have to be, the bound alone decides.
No kernel may reach another device: no remote copies, remote signals or barrier semaphores. Data moves between devices by JAX's collectives and lax.ppermute only.
A program may use at most 64 MiB of HBM per device.

v0:
```python
import jax
import jax.numpy as jnp
from jax import lax
from jax.sharding import Mesh
from jax.sharding import PartitionSpec as P

P_SIZE = 4096
GX_GY_GZ = ("gx", "gy", "gz_0", "gz_1")
GY_GZ = ("gy", "gz_0", "gz_1")
STRENGTH = 20.0
S_HOME = 0.5
KAPPA_S = 0.5
KAPPA_Z = 0.05
PAIR_SCALE = 0.02
WIDTH_SQ = 4.0


def one_axis_at_a_time(array, axes):
    for axis in axes:
        array = lax.psum(array, axis)
    return array


def pair_block(block_pos, all_pos):
    diff = block_pos[:, :, None] - all_pos[:, None, :]
    dist_sq = jnp.sum(diff * diff, axis=0)
    weight = PAIR_SCALE * jnp.exp(-dist_sq / WIDTH_SQ)
    return jnp.sum(weight[None] * diff, axis=2)


def domain_forces(local):
    atoms = local.shape[1]
    rows = 256
    blocks = local.reshape(3, atoms // rows, rows).transpose(1, 0, 2)
    result = lax.map(lambda block: pair_block(block, local), blocks)
    return result.transpose(1, 0, 2).reshape(3, atoms)


def slot_ids(path_count, path_order, slots):
    offsets = jnp.cumsum(path_count) - path_count
    steps_k = jnp.arange(slots, dtype=jnp.int32)
    live = steps_k[None, :] < path_count[:, None]
    place = jnp.clip(offsets[:, None] + steps_k[None, :], 0, P_SIZE - 1)
    ids = jnp.where(live, path_order[place], -1)
    return (ids, live)


def cv_terms(dist, frame_rank):
    frames_n = dist.shape[0]
    expo = -STRENGTH * dist
    top = jnp.max(expo)
    expd = jnp.exp(expo - top)
    total = jnp.sum(expd)
    weight = expd / total
    progress_rank = frame_rank.astype(jnp.float32) / (frames_n - 1.0)
    s_value = jnp.sum(progress_rank * weight)
    z_value = -(top + jnp.log(total)) / STRENGTH
    grads = (
        KAPPA_S * P_SIZE * (s_value - S_HOME) * -STRENGTH * weight * (progress_rank - s_value)
        + KAPPA_Z * P_SIZE * z_value * weight
    )
    return (s_value, z_value, grads)


def summed_terms(partial_value, frame_rank):
    dist = one_axis_at_a_time(partial_value, GX_GY_GZ)
    return cv_terms(dist, frame_rank)


def body(positions, frames, path_slot, path_count, path_order, frame_rank):
    slots = path_slot.shape[1]
    local_slot = path_slot[0]
    ids, live = slot_ids(path_count, path_order, slots)
    path_pos = jnp.take(positions, local_slot, axis=1)
    here = lax.axis_index(GX_GY_GZ)
    my_ids = lax.dynamic_slice_in_dim(ids, here, 1, 0)[0]
    mask = lax.dynamic_slice_in_dim(live, here, 1, 0)[0].astype(jnp.float32)
    whole = lax.all_gather(frames, GY_GZ, axis=2, tiled=True)
    refs = jnp.take(whole, jnp.clip(my_ids, 0, P_SIZE - 1), axis=2)
    delta = path_pos[None] - refs
    partial_value = jnp.sum(jnp.sum(delta * delta, axis=1) * mask[None], axis=1) / P_SIZE
    s_value, z_value, grads = summed_terms(partial_value, frame_rank)
    bias = (
        -(2.0 / P_SIZE)
        * jnp.einsum("f,fcm->cm", grads, delta, precision=lax.Precision.HIGHEST)
        * mask[None]
    )
    forces = domain_forces(positions)
    forces = forces.at[:, local_slot].add(bias)
    return (forces, jnp.stack([s_value, z_value]))


def solution(mesh):
    finer = Mesh(
        mesh.devices.reshape(mesh.shape["gx"], mesh.shape["gy"], 8, 2), ("gx", "gy", "gz_0", "gz_1")
    )
    return jax.shard_map(
        body,
        mesh=finer,
        in_specs=(P(None, GX_GY_GZ), P(None, None, GY_GZ), P(GX_GY_GZ, None), P(), P(), P()),
        out_specs=(P(None, GX_GY_GZ), P()),
        check_vma=False,
    )
```

profile of v0, /device:TPU:1, one launch (start us, length us, event | category | flops | bytes accessed | tf_op | source)
XLA Modules:
  0.0 190.1 jit_solution(15374449258505947878)
XLA Ops:
  7.2 0.0 copy-start
  7.2 0.0 all-gather.2.cloned.1.call-start
  7.2 0.7 all-gather.2.cloned.1.call-update
  7.9 1.0 reduce-window.9
  8.9 0.1 slice.7
  9.0 0.1 slice_reduce_fusion
  9.1 0.8 bitcast_subtract_fusion.1
  9.9 0.1 compare_select_fusion
  10.0 0.1 reshape.176
  10.2 0.0 copy-done
  10.2 0.0 copy-start.1
  10.2 90.5 %gather_fusion.1 = s32[16384]{0:T(1024)S(1)} fusion(s32[4096]{0:T(1024)S(1)} %copy-done, s32[16384]{0:T(1024)S(1)} %broadcast_clamp_fusion), kind=kCustom, calls=%fused_computation.1 | custom fusion | bytes 196608 | tf_op jit(solution)/shard_map/gather | solution.py:44
  100.8 0.1 reshape.175
  100.9 0.0 copy-done.1
  100.9 0.1 copy.21
  101.0 0.0 copy-start.4
  101.0 0.0 copy-start.2
  101.1 1.5 while.10
  101.1 0.2 fusion.25
  101.3 0.1 exponential_multiply_fusion.2
  101.4 0.4 fusion.26
  101.8 0.2 fusion.25
  102.0 0.1 exponential_multiply_fusion.2
  102.1 0.4 fusion.26
  102.5 0.1 copy.20
  102.7 0.0 copy-done.4
  102.7 0.6 gather_fusion
  103.3 0.0 copy-done.2
  103.3 0.1 iota_compare_fusion
  103.5 0.1 select_bitcast_fusion
  103.6 0.0 copy-start.3
  103.6 0.0 all-gather.2.cloned.1.call-done
  103.6 10.7 %copy.22 = f32[128,3,4096]{0,1,2:T(4,128)} copy(f32[128,3,4096]{0,2,1:T(8,128)} %all-gather.2.cloned.1.call-done) | data formatting | bytes 12582912 | tf_op jit(solution)/shard_map/all_gather | solution.py:78
  114.3 4.0 %gather_fusion.2 = f32[32,128,3]{1,2,0:T(4,128)S(1)} fusion(f32[128,3,4096]{0,1,2:T(4,128)} %copy.22, s32[1024]{0:T(1024)S(1)} %pad_clamp_fusion), kind=kCustom, calls=%fused_computation.2 | custom fusion | bytes 98432 | tf_op jit(solution)/shard_map/jit(_take)/gather | solution.py:79
  118.3 0.1 multiply_reduce_fusion
  118.4 0.1 multiply_reduce_fusion.1
  118.5 9.3 %psum.28 = f32[128]{0:T(128)S(1)} all-reduce(f32[128]{0:T(128)S(1)} %broadcast_multiply_fusion), channel_id=1, replica_groups=mesh['gx'=4,'gy'=8,'gz_0'=8,'gz_1'=2] {'gx'}, use_global_device_ids=true, to_apply=%region_8.9 | all-reduce | flops 128 | bytes 1024 | tf_op jit(solution)/shard_map/psum | solution.py:20
  127.8 19.5 %psum.29 = f32[128]{0:T(128)S(1)} all-reduce(f32[128]{0:T(128)S(1)} %psum.28), channel_id=1, replica_groups=mesh['gx'=4,'gy'=8,'gz_0'=8,'gz_1'=2] {'gy'}, use_global_device_ids=true, to_apply=%region_9.10 | all-reduce | flops 128 | bytes 1024 | tf_op jit(solution)/shard_map/psum | solution.py:20
  147.3 13.8 %psum.30 = f32[128]{0:T(128)S(1)} all-reduce(f32[128]{0:T(128)S(1)} %psum.29), channel_id=1, replica_groups=mesh['gx'=4,'gy'=8,'gz_0'=8,'gz_1'=2] {'gz_0'}, use_global_device_ids=true, to_apply=%region_10.11 | all-reduce | flops 128 | bytes 1024 | tf_op jit(solution)/shard_map/psum | solution.py:20
  161.1 12.3 %psum.31 = f32[128]{0:T(128)S(1)} all-reduce(f32[128]{0:T(128)S(1)} %psum.30), channel_id=1, replica_groups=mesh['gx'=4,'gy'=8,'gz_0'=8,'gz_1'=2] {'gz_1'}, use_global_device_ids=true, to_apply=%region_11.12 | all-reduce | flops 128 | bytes 1024 | tf_op jit(solution)/shard_map/psum | solution.py:20
  173.4 0.6 multiply_reduce_fusion.3
  174.0 1.3 fusion.21
  176.6 0.0 copy-done.3
  176.6 2.0 %multiply_reduce_fusion.2 = (f32[]{:T(128)}, f32[128]{0:T(128)S(1)}) fusion(s32[128]{0:T(128)S(1)} %copy-done.3, f32[]{:T(128)} %fusion.21, f32[]{:T(128)} %multiply_reduce_fusion.3, f32[128]{0:T(128)S(1)} %psum.31), kind=kLoop, calls=%fused_computation.47 | loop fusion | flops 895 | bytes 1548 | tf_op jit(solution)/shard_map/reduce_sum | solution.py:56
  179.3 0.9 fusion.2
  180.2 0.1 copy.25
  180.3 1.0 scatter_custom_fusion
  181.3 0.7 copy.23
  182.0 1.3 pad_maximum_fusion
  (15 shorter events, 0.2 us)
Async XLA Ops:
  7.2 3.0 %copy-start = (s32[4096]{0:T(1024)S(1)}, s32[4096]{0:T(1024)}, u32[]{:S(2)}) copy-start(s32[4096]{0:T(1024)} %param.12) | copy-start | bytes 49156
  7.2 96.4 %all-gather.2.cloned.1.call-start = ((), (), s32[]{:S(2)}) async-start(), calls=%async_computation | async-start | bytes 6340608 | tf_op jit(solution)/shard_map/all_gather | solution.py:78
  10.2 90.7 %copy-start.1 = (f32[3,512]{1,0:T(4,128)S(1)}, f32[3,512]{1,0:T(4,128)}, u32[]{:S(2)}) copy-start(f32[3,512]{1,0:T(4,128)} %param.8) | copy-start | bytes 18436
  101.0 1.6 copy-start.4
  101.0 2.2 %copy-start.2 = (s32[512]{0:T(512)S(1)}, s32[512]{0:T(512)}, u32[]{:S(2)}) copy-start(s32[512]{0:T(512)} %param.11) | copy-start | bytes 6148
  103.6 73.0 %copy-start.3 = (s32[128]{0:T(128)S(1)}, s32[128]{0:T(128)}, u32[]{:S(2)}) copy-start(s32[128]{0:T(128)} %param.13) | copy-start | bytes 1540
Sparse Core Ops, SparseCore 0:
  11.2 91.8 all-gather.1
where the time goes:
time: 191 us; the launch traced here: 190 us
  local copies, waits for them, and re-layouts  107 us (56%)
  blocking collectives  54.9 us (29%)
  between operations  16.3 us (9%)
  other arithmetic  9.86 us (5%)
    gather x2, local copies, waits for them, and re-layouts, slot_ids(): ids = jnp.where(live, path_order[place], -1)  90.7 us
    psum x4, blocking collectives, one_axis_at_a_time(): array = lax.psum(array, axis)  54.9 us
    all_gather x1, local copies, waits for them, and re-layouts, body(): whole = lax.all_gather(frames, GY_GZ, axis=2, tiled=True)  10.7 us
    gather x1, local copies, waits for them, and re-layouts, body(): refs = jnp.take(whole, jnp.clip(my_ids, 0, P_SIZE - 1), axis=2)  3.99 us
  transfers between devices with their start and end apart: 1, of which 0 were waited for; matrix products, arithmetic and copies ran while one was open for 50% of the time, Pallas kernels for 0%

commit v1 on v0

--- a/solution.py
+++ b/solution.py
@@ -75,7 +75,11 @@
     here = lax.axis_index(GX_GY_GZ)
     my_ids = lax.dynamic_slice_in_dim(ids, here, 1, 0)[0]
     mask = lax.dynamic_slice_in_dim(live, here, 1, 0)[0].astype(jnp.float32)
-    whole = lax.all_gather(frames, GY_GZ, axis=2, tiled=True)
+    choose_edges = lambda m, in_dim: jnp.concatenate(
+        jax.lax.all_to_all(jnp.stack([m for _ in range(jax.lax.axis_size(GY_GZ))]), GY_GZ, 0, 0),
+        in_dim,
+    )
+    whole = choose_edges(frames, in_dim=2)
     refs = jnp.take(whole, jnp.clip(my_ids, 0, P_SIZE - 1), axis=2)
     delta = path_pos[None] - refs
     partial_value = jnp.sum(jnp.sum(delta * delta, axis=1) * mask[None], axis=1) / P_SIZE

time: 191 us -> 280 us (1.47)
  waiting for transfers between devices: 0.68 us -> 67.5 us
  starting transfers between devices: 0.04 us -> 18.9 us
  local copies, waits for them, and re-layouts: 107 us -> 123 us
  between operations: 16.3 us -> 2.92 us
    all_to_all x0 -> x1, waiting for transfers between devices: none -> 67.5 us  [body(): jax.lax.all_to_all(jnp.stack([m for _ in range(jax.lax.axis_size(GY_GZ))]...]
    all_to_all x0 -> x1, starting transfers between devices: none -> 18.9 us  [body(): jax.lax.all_to_all(jnp.stack([m for _ in range(jax.lax.axis_size(GY_GZ))]...]
    reshape x0 -> x1, local copies, waits for them, and re-layouts: none -> 18.7 us  [body(): jnp.concatenate(jax.lax.all_to_all(jnp.stack([m for _ in range(jax.lax.ax...]
    all_gather x1 -> x0, local copies, waits for them, and re-layouts: 10.7 us -> none  [body(): whole = lax.all_gather(frames, GY_GZ, axis=2, tiled=True)]
    another operation x1 -> x2, local copies, waits for them, and re-layouts: 0.12 us -> 4.38 us  [the longest x1 4.26 us: body(): jnp.stack([m for _ in range(jax.lax.axis_size(GY_GZ))])]
    all_to_all x0 -> x1, local copies, waits for them, and re-layouts: none -> 3.49 us  [body(): jax.lax.all_to_all(jnp.stack([m for _ in range(jax.lax.axis_size(GY_GZ))]...]
  transfers between devices with their start and end apart: 1 -> 1, of which waited for: 0 -> 1; matrix products, arithmetic and copies ran while one was open for 50% -> 34% of each run, Pallas kernels for 0% -> 0%
where the time goes in v1:
time: 280 us; the launch traced here: 279 us
  local copies, waits for them, and re-layouts  123 us (44%)
  waiting for transfers between devices  67.5 us (24%)
  blocking collectives  57.5 us (21%)
  starting transfers between devices  18.9 us (7%)
  other arithmetic  8.5 us (3%)
  between operations  2.92 us (1%)
    gather x2, local copies, waits for them, and re-layouts, slot_ids(): ids = jnp.where(live, path_order[place], -1)  90.7 us
    all_to_all x1, waiting for transfers between devices, body(): jax.lax.all_to_all(jnp.stack([m for _ in range(jax.lax.axis_size(GY_GZ))]...  67.5 us
    psum x4, blocking collectives, one_axis_at_a_time(): array = lax.psum(array, axis)  57.5 us
    all_to_all x1, starting transfers between devices, body(): jax.lax.all_to_all(jnp.stack([m for _ in range(jax.lax.axis_size(GY_GZ))]...  18.9 us
    reshape x1, local copies, waits for them, and re-layouts, body(): jnp.concatenate(jax.lax.all_to_all(jnp.stack([m for _ in range(jax.lax.ax...  18.7 us
  transfers between devices with their start and end apart: 1, of which 1 were waited for; matrix products, arithmetic and copies ran while one was open for 34% of the time, Pallas kernels for 0%

profile of v1, /device:TPU:1, one launch (start us, length us, event | category | flops | bytes accessed | tf_op | source)
XLA Modules:
  0.0 279.4 jit_solution(13632184589611578478)
XLA Ops:
  0.6 0.0 copy-start
  0.6 4.3 %stack.8 = f32[128,128,3,32]{1,3,2,0:T(8,128)} broadcast(f32[128,3,32]{0,2,1:T(8,128)} %param.9), dimensions={1,2,3} | broadcast | bytes 6340608 | tf_op jit(solution)/shard_map/stack | solution.py:79
  4.9 0.0 copy-start.2
  4.9 18.9 %all-to-all-start = ((f32[128,128,3,32]{1,3,2,0:T(8,128)}), f32[128,128,3,32]{1,3,2,0:T(8,128)}, u32[]{:S(2)}, u32[]{:S(2)}) async-start(f32[128,128,3,32]{1,3,2,0:T(8,128)} %stack.8), calls=%async_computation | async-start | bytes 12582912 | tf_op jit(solution)/shard_map/all_to_all | solution.py:79
  23.9 0.0 copy-done.2
  23.9 0.3 reduce-window.9
  24.2 0.1 slice.7
  24.3 0.1 slice_reduce_fusion
  24.4 0.1 bitcast_subtract_fusion.1
  24.5 0.1 compare_select_fusion
  24.6 0.1 reshape.186
  24.8 0.0 copy-done
  24.8 0.0 copy-start.1
  24.8 90.5 %gather_fusion.1 = s32[16384]{0:T(1024)S(1)} fusion(s32[4096]{0:T(1024)S(1)} %copy-done, s32[16384]{0:T(1024)S(1)} %broadcast_clamp_fusion), kind=kCustom, calls=%fused_computation.1 | custom fusion | bytes 196608 | tf_op jit(solution)/shard_map/gather | solution.py:44
  115.4 0.1 reshape.185
  115.5 0.0 copy-done.1
  115.5 0.1 copy.23
  115.6 0.0 copy-start.4
  115.7 1.4 while.10
  115.7 0.2 fusion.25
  115.9 0.1 exponential_multiply_fusion.2
  116.0 0.4 fusion.26
  116.4 0.2 fusion.25
  116.6 0.1 exponential_multiply_fusion.2
  116.7 0.4 fusion.26
  117.1 0.1 copy.22
  117.3 0.0 copy-done.4
  117.3 0.6 gather_fusion
  117.9 0.1 iota_compare_fusion
  118.1 0.1 select_bitcast_fusion
  118.2 67.5 %all-to-all-done = f32[128,128,3,32]{1,3,2,0:T(8,128)} async-done(((f32[128,128,3,32]{1,3,2,0:T(8,128)}), f32[128,128,3,32]{1,3,2,0:T(8,128)}, u32[]{:S(2)}, u32[]{:S(2)}) %all-to-all-start) | async-done | bytes 6291488 | tf_op jit(solution)/shard_map/all_to_all | solution.py:79
  185.6 3.5 %copy.24 = f32[128,128,3,32]{1,3,0,2:T(8,128)S(1)} copy(f32[128,128,3,32]{1,3,2,0:T(8,128)} %all-to-all-done) | data formatting | bytes 12582912 | tf_op jit(solution)/shard_map/all_to_all | solution.py:79
  189.1 0.0 copy-start.3
  189.1 18.7 %copy.25 = f32[128,3,4096]{0,1,2:T(4,128)} copy(f32[128,3,4096]{0,2,1:T(8,128)S(1)} %bitcast.55) | data formatting | bytes 12582912 | tf_op jit(solution)/shard_map/reshape | solution.py:78
  207.8 4.0 %gather_fusion.2 = f32[32,128,3]{1,2,0:T(4,128)S(1)} fusion(f32[128,3,4096]{0,1,2:T(4,128)} %copy.25, s32[1024]{0:T(1024)S(1)} %pad_clamp_fusion), kind=kCustom, calls=%fused_computation.2 | custom fusion | bytes 98432 | tf_op jit(solution)/shard_map/jit(_take)/gather | solution.py:83
  211.8 0.1 multiply_reduce_fusion
  212.0 0.1 multiply_reduce_fusion.1
  212.0 8.5 %psum.28 = f32[128]{0:T(128)S(1)} all-reduce(f32[128]{0:T(128)S(1)} %broadcast_multiply_fusion), channel_id=1, replica_groups=mesh['gx'=4,'gy'=8,'gz_0'=8,'gz_1'=2] {'gx'}, use_global_device_ids=true, to_apply=%region_8.9 | all-reduce | flops 128 | bytes 1024 | tf_op jit(solution)/shard_map/psum | solution.py:20
  220.5 16.3 %psum.29 = f32[128]{0:T(128)S(1)} all-reduce(f32[128]{0:T(128)S(1)} %psum.28), channel_id=1, replica_groups=mesh['gx'=4,'gy'=8,'gz_0'=8,'gz_1'=2] {'gy'}, use_global_device_ids=true, to_apply=%region_9.10 | all-reduce | flops 128 | bytes 1024 | tf_op jit(solution)/shard_map/psum | solution.py:20
  236.8 20.3 %psum.30 = f32[128]{0:T(128)S(1)} all-reduce(f32[128]{0:T(128)S(1)} %psum.29), channel_id=1, replica_groups=mesh['gx'=4,'gy'=8,'gz_0'=8,'gz_1'=2] {'gz_0'}, use_global_device_ids=true, to_apply=%region_10.11 | all-reduce | flops 128 | bytes 1024 | tf_op jit(solution)/shard_map/psum | solution.py:20
  257.1 12.5 %psum.31 = f32[128]{0:T(128)S(1)} all-reduce(f32[128]{0:T(128)S(1)} %psum.30), channel_id=1, replica_groups=mesh['gx'=4,'gy'=8,'gz_0'=8,'gz_1'=2] {'gz_1'}, use_global_device_ids=true, to_apply=%region_11.12 | all-reduce | flops 128 | bytes 1024 | tf_op jit(solution)/shard_map/psum | solution.py:20
  269.6 0.6 multiply_reduce_fusion.3
  270.2 1.3 fusion.21
  272.8 0.0 copy-done.3
  272.8 2.0 multiply_reduce_fusion.2
  275.5 0.9 fusion.2
  276.4 0.1 copy.28
  276.5 1.0 scatter_custom_fusion
  277.5 0.7 copy.26
  278.2 1.3 pad_maximum_fusion
  (15 shorter events, 0.2 us)
Async XLA Ops:
  0.6 24.2 %copy-start = (s32[4096]{0:T(1024)S(1)}, s32[4096]{0:T(1024)}, u32[]{:S(2)}) copy-start(s32[4096]{0:T(1024)} %param.12) | copy-start | bytes 49156
  4.9 19.0 %copy-start.2 = (s32[512]{0:T(512)S(1)}, s32[512]{0:T(512)}, u32[]{:S(2)}) copy-start(s32[512]{0:T(512)} %param.11) | copy-start | bytes 6148
  4.9 180.7 %all-to-all-start = ((f32[128,128,3,32]{1,3,2,0:T(8,128)}), f32[128,128,3,32]{1,3,2,0:T(8,128)}, u32[]{:S(2)}, u32[]{:S(2)}) async-start(f32[128,128,3,32]{1,3,2,0:T(8,128)} %stack.8), calls=%async_computation | async-start | bytes 12582912 | tf_op jit(solution)/shard_map/all_to_all | solution.py:79
  24.8 90.7 %copy-start.1 = (f32[3,512]{1,0:T(4,128)S(1)}, f32[3,512]{1,0:T(4,128)}, u32[]{:S(2)}) copy-start(f32[3,512]{1,0:T(4,128)} %param.8) | copy-start | bytes 18436
  115.6 1.6 copy-start.4
  189.1 83.6 %copy-start.3 = (s32[128]{0:T(128)S(1)}, s32[128]{0:T(128)}, u32[]{:S(2)}) copy-start(s32[128]{0:T(128)} %param.13) | copy-start | bytes 1540
